TPU v7x, 256 devices: a whole 4x4x8 slice. The times are simulated.
256 devices in a mesh: rep: 2 (over core), dp: 128 (over x, y, z).
Axes of the slice: x: 4, y: 4, z: 8, core: 2. Of those that a mesh axis runs over, the one named last changes fastest.
Arguments:
- a: bfloat16 [256, 2, 4096, 640], P(('rep', 'dp')), parts along dimension 0
- g: bfloat16 [256, 2, 4096, 2048], P(('rep', 'dp')), parts along dimension 0
Outputs:
- output: bfloat16 [4, 640, 2048], P('rep'), parts along dimension 0
There are 2 independent parts. A program takes and returns all parts, laid end to end along the dimension named above; each array names one.
All inputs are finite; a program needn't handle non-finite values.
Results may differ from a plain program's by a relative error of at most 0.012.
Values are sent between devices in bfloat16 or wider.
A program may use at most 768 MiB of HBM per device.

v0:
```python
import jax
import jax.numpy as jnp


def solution(mesh):
    groups = mesh.shape["rep"]

    def step(a, g):
        a, g = (t.reshape(groups, -1, *t.shape[1:]) for t in (a, g))
        sums = jnp.einsum("rsntd,rsntf->rndf", a, g, preferred_element_type=jnp.float32)
        return sums.astype(jnp.bfloat16).reshape(-1, *sums.shape[2:])

    return step
```

profile of v0, /device:TPU:0, one launch (start us, length us, event | category | flops | bytes accessed | tf_op | source)
XLA Modules:
  0.0 827.9 jit_solution(11368749422713937173)
XLA Ops:
  0.0 29.4 %fusion.3 = f32[1,2,640,2048]{3,2,1,0:T(8,128)} fusion(bf16[1,2,4096,2048]{3,2,1,0:T(8,128)(2,1)} %param.1, bf16[1,2,4096,640]{3,2,1,0:T(8,128)(2,1)} %param), kind=kOutput, calls=%fused_computation.4 | convolution fusion | flops 21474836480 | bytes 54525952 | tf_op jit(solution)/rsntd,rsntf->rndf/dot_general | solution.py:10
  29.4 798.5 %all-reduce.2 = bf16[1,2,640,2048]{3,2,1,0:T(8,128)(2,1)} all-reduce(f32[1,2,640,2048]{3,2,1,0:T(8,128)} %fusion.3), channel_id=1, replica_groups=[2,128]<=[256], use_global_device_ids=true, to_apply=%add.clone | all-reduce | flops 2621440 | bytes 15728640 | tf_op jit(solution)/rsntd,rsntf->rndf/dot_general | solution.py:10
where the time goes:
time: 828 us
  blocking collectives  798 us (96%)
  matrix products  29.4 us (4%)
    dot_general x1, blocking collectives, step(): jnp.einsum('rsntd,rsntf->rndf', a, g, preferred_element_type=jnp.float32)  798 us
    dot_general x1, matrix products, step(): jnp.einsum('rsntd,rsntf->rndf', a, g, preferred_element_type=jnp.float32)  29.4 us

commit v1 on v0

v1 whole, which is shorter than its diff:
```python
import functools

import jax
import jax.numpy as jnp
from jax import lax
from jax.experimental import pallas as pl
from jax.experimental.pallas import tpu as pltpu
from jax.sharding import PartitionSpec as P

X, Y, Z = 4, 4, 8
TOKENS, D, FF = 4096, 640, 2048
W = 1024
CW = 512
KB = 1024
SLOTS = 3
BF, F32 = jnp.bfloat16, jnp.float32

PLANS = (
    (("x", 0, 256), ("y", 256, 256), ("z", 512, 128)),
    (("x", 0, 256), ("z", 256, 256), ("y", 512, 128)),
    (("y", 0, 256), ("z", 256, 256), ("x", 512, 128)),
    (("x", 0, 256), ("y", 256, 256), ("z", 512, 128)),
)
CHUNKS = len(PLANS)
SEMS_XY, SEMS_Z = 30, 52


def scratch_of(colour, rows):
    if colour == "z":
        s = rows // Z
        return [
            pltpu.VMEM((14, s, W // 2), BF),
            pltpu.VMEM((16, s // 2, 128), BF),
            pltpu.VMEM((15, s // 2, 128), BF),
        ]
    s = rows // 4
    return [
        pltpu.VMEM((6, s // 2, W), BF),
        pltpu.VMEM((4, s // 4, W), BF),
        pltpu.VMEM((3, s // 4, W), BF),
        pltpu.VMEM((8, s // 4, 128), BF),
        pltpu.VMEM((7, s // 4, 128), BF),
    ]


class Place:
    def __init__(self):
        me = lax.axis_index("dp")
        self.first = lax.axis_index("rep") * (X * Y * Z)
        self.pos = {"x": lax.div(me, Y * Z), "y": lax.rem(lax.div(me, Z), Y), "z": lax.rem(me, Z)}
        self.spot = lax.div(me, Z)
        size = {"x": X, "y": Y, "z": Z}
        self.at = {(k, d): lax.rem(self.pos[k] + d, size[k]) if d else self.pos[k] for k in size for d in range(size[k])}
        self.plane, self.peers = {}, {}
        for dx in range(X):
            for dy in range(Y):
                self.plane[dx, dy] = self.at["x", dx] * Y + self.at["y", dy]
                self.peers[dx, dy, 0] = self.first + self.plane[dx, dy] * Z + self.pos["z"]
        for d in range(1, Z):
            self.peers[0, 0, d] = self.first + self.spot * Z + self.at["z", d]
        del self.peers[0, 0, 0]

    def peer(self, x=0, y=0, z=0):
        return self.peers[x % X, y % Y, z % Z]


class Links:
    def __init__(self, place, send_sems, recv_sems):
        self.place, self.pos, self.at = place, place.pos, place.at
        self.send_sems, self.recv_sems = send_sems, recv_sems
        self.next = 0

    def send(self, src, dst, **steps):
        i = self.next
        self.next += 1
        copy = pltpu.make_async_remote_copy(
            src_ref=src,
            dst_ref=dst,
            send_sem=self.send_sems.at[i],
            recv_sem=self.recv_sems.at[i],
            device_id=self.place.peer(**steps),
            device_id_type=pl.DeviceIdType.LOGICAL,
        )
        copy.start()
        return copy


def f32(value):
    return value.astype(F32)


def stream_xy(links, axis, other, term, out, n, col0, row0, rows, bufs):
    ra, a1, rb, a2, rc = bufs
    s, h, q = rows // 4, rows // 8, rows // 16
    p, pb, pz = links.pos[axis], links.pos[other], links.pos["z"]
    nxt, prv, far = links.at[axis, 1], links.at[axis, 3], links.at[axis, 2]
    sent = []

    def piece(j, half):
        return term.at[pl.ds(pl.multiple_of(row0 + j * s + half * h, 8), h), :]

    def go(src, dst, **steps):
        sent.append(links.send(src, dst, **steps))
        return sent[-1]

    up, down = {axis: 1}, {axis: -1}
    m0 = go(piece(far, 0), ra.at[0], **up)
    w0 = go(piece(far, 1), ra.at[3], **down)
    m1 = go(piece(nxt, 1), ra.at[1], **up)
    w1 = go(piece(prv, 0), ra.at[4], **down)
    yield
    m0.wait_recv()
    there = piece(nxt, 0)
    there[...] = (f32(there[...]) + f32(ra[0])).astype(BF)
    m2 = go(there, ra.at[2], **up)
    w0.wait_recv()
    there = piece(prv, 1)
    there[...] = (f32(there[...]) + f32(ra[3])).astype(BF)
    w2 = go(there, ra.at[5], **down)
    yield
    w1.wait_recv()
    m2.wait_recv()
    total = f32(piece(p, 0)[...]) + f32(ra[2]) + f32(ra[4])
    total = total.astype(BF)
    a1[0] = total[:q]
    a1[1] = total[q:]
    m1.wait_recv()
    w2.wait_recv()
    total = f32(piece(p, 1)[...]) + f32(ra[1]) + f32(ra[5])
    total = total.astype(BF)
    a1[2] = total[:q]
    a1[3] = total[q:]
    got = [go(a1.at[links.at[other, d]], rb.at[d - 1], **{other: d}) for d in (2, 1, 3)]
    yield
    for copy in got:
        copy.wait_recv()
    total = f32(a1[pb]) + f32(rb[0]) + f32(rb[1]) + f32(rb[2])
    total = total.astype(BF)
    for j in range(8):
        a2[j] = total[:, j * 128 : (j + 1) * 128]
    got = [go(a2.at[links.at["z", d]], rc.at[d - 1], z=d) for d in (4, 3, 5, 2, 6, 1, 7)]
    yield
    for copy in got:
        copy.wait_recv()
    total = f32(a2[pz])
    for d in range(7):
        total = total + f32(rc[d])
    row = pl.multiple_of(row0 + p * s + pb * q, 8)
    tile = out.at[n, pl.ds(row, q), pl.ds(pl.multiple_of(col0 + pz * 128, 128), 128)]
    tile[...] = total.astype(BF)
    got = [go(tile, tile, z=d) for d in (4, 3, 5, 2, 6, 1, 7)]
    yield
    for copy in got:
        copy.wait_recv()
    cols = pl.ds(col0, W)
    block = out.at[n, pl.ds(row, q), cols]
    got = [go(block, block, **{other: d}) for d in (2, 1, 3)]
    yield
    for copy in got:
        copy.wait_recv()
    shard = out.at[n, pl.ds(pl.multiple_of(row0 + p * s, 8), s), cols]
    g0, g1 = go(shard, shard, **up), go(shard, shard, **down)
    yield
    g0.wait_recv()
    half = out.at[n, pl.ds(pl.multiple_of(row0 + prv * s, 8), h), cols]
    g2 = go(half, half, **up)
    g1.wait_recv()
    half = out.at[n, pl.ds(pl.multiple_of(row0 + nxt * s + h, 8), h), cols]
    g3 = go(half, half, **down)
    yield
    for copy in sent:
        copy.wait_send()
    g2.wait_recv()
    g3.wait_recv()


def stream_z(links, term, out, n, col0, row0, rows, bufs):
    rz, az, rp = bufs
    s, hc = rows // 8, W // 2
    p = links.pos["z"]
    spot = links.place.spot
    sent = []

    def piece(j, half):
        return term.at[pl.ds(pl.multiple_of(row0 + j * s, 8), s), pl.ds(half * hc, hc)]

    def go(src, dst, **steps):
        sent.append(links.send(src, dst, **steps))
        return sent[-1]

    chains = ((1, 0, 4), (-1, 1, 4), (1, 1, 3), (-1, 0, 3))
    slot, last = 0, {}
    for t in range(4):
        for way, half, length in chains:
            if t >= length:
                continue
            there = piece(links.at["z", way * (length - t) % Z], half)
            if t:
                copy, buf = last[way, half]
                copy.wait_recv()
                there[...] = (f32(there[...]) + f32(rz[buf])).astype(BF)
            last[way, half] = go(there, rz.at[slot], z=way), slot
            slot += 1
        yield
    for half in range(2):
        total = f32(piece(p, half)[...])
        for way in (1, -1):
            copy, buf = last[way, half]
            copy.wait_recv()
            total = total + f32(rz[buf])
        total = total.astype(BF)
        for c in range(4):
            for r in range(2):
                az[r * 8 + half * 4 + c] = total[r * (s // 2) : (r + 1) * (s // 2), c * 128 : (c + 1) * 128]
    steps = sorted(((dx, dy) for dx in range(X) for dy in range(Y) if dx or dy), key=lambda v: -min(v[0], X - v[0]) - min(v[1], Y - v[1]))
    got = []
    for i, (dx, dy) in enumerate(steps):
        got.append(go(az.at[links.place.plane[dx, dy]], rp.at[i], x=dx, y=dy))
    yield
    for copy in got:
        copy.wait_recv()
    total = f32(az[spot])
    for i in range(15):
        total = total + f32(rp[i])
    row = pl.multiple_of(row0 + p * s + lax.div(spot, 8) * (s // 2), 8)
    col = pl.multiple_of(col0 + lax.rem(spot, 8) * 128, 128)
    tile = out.at[n, pl.ds(row, s // 2), pl.ds(col, 128)]
    tile[...] = total.astype(BF)
    got = [go(tile, tile, x=dx, y=dy) for dx, dy in steps]
    yield
    for copy in got:
        copy.wait_recv()

    def shard(j, half=None):
        r = pl.ds(pl.multiple_of(row0 + j * s, 8), s)
        return out.at[n, r, pl.ds(col0, W) if half is None else pl.ds(col0 + half * hc, hc)]

    mine = shard(p)
    g0, g1 = go(mine, mine, z=1), go(mine, mine, z=-1)
    yield
    for t in (1, 2, 3):
        g0.wait_recv()
        there = shard(links.at["z", Z - t], 0 if t == 3 else None)
        h0 = go(there, there, z=1)
        g1.wait_recv()
        there = shard(links.at["z", t], 1 if t == 3 else None)
        h1 = go(there, there, z=-1)
        g0, g1 = h0, h1
        yield
    for copy in sent:
        copy.wait_send()
    g0.wait_recv()
    g1.wait_recv()


def kernel(compute, comm, a_hbm, g_hbm, out, av, gv, at, acc, term, a_sem, g_sem, *rest):
    bufs, sems = rest[: -2 * 3 * CHUNKS], rest[-2 * 3 * CHUNKS :]
    blocks, per, steps = 2 * FF // CW, FF // CW, TOKENS // KB

    def a_copy(n, k):
        rows = pl.ds(k * KB, KB)
        return pltpu.make_async_copy(a_hbm.at[0, n, rows], av.at[n, rows], a_sem.at[n, k])

    def g_copy(b, k):
        rows = pl.ds(k * KB, KB)
        src = g_hbm.at[0, b // per, rows, pl.ds((b % per) * CW, CW)]
        return pltpu.make_async_copy(src, gv.at[b % SLOTS, rows], g_sem.at[b % SLOTS, k])

    if comm:
        barrier = pltpu.get_barrier_semaphore()
        place = Place()
        for peer in place.peers.values():
            pl.semaphore_signal(barrier, inc=1, device_id=peer, device_id_type=pl.DeviceIdType.LOGICAL)
    if compute:
        for k in range(steps):
            a_copy(0, k).start()
            g_copy(0, k).start()
        for b in range(1, SLOTS):
            for k in range(steps):
                g_copy(b, k).start()
        for k in range(steps):
            a_copy(1, k).start()

    active = []

    def tick():
        for stream in list(active):
            if next(stream, "end") == "end":
                active.remove(stream)

    for b in range(blocks):
        n = b // per
        c = b * CW // W
        off = (b * CW) % W
        if compute:
            for k in range(steps):
                rows = pl.ds(k * KB, KB)
                if b % per == 0:
                    a_copy(n, k).wait()
                    at[:, rows] = av[n, rows, :].T
                g_copy(b, k).wait()
                part = jnp.dot(at[:, rows], gv[b % SLOTS, rows, :], preferred_element_type=F32)
                if k == 0:
                    acc[...] = part
                elif k < steps - 1:
                    acc[...] += part
                else:
                    term[c, :, off : off + CW] = (acc[...] + part).astype(BF)
            if b + SLOTS < blocks:
                for k in range(steps):
                    g_copy(b + SLOTS, k).start()
        if not comm:
            continue
        if b == W // CW - 1:
            pl.semaphore_wait(barrier, len(place.peers))
        tick()
        if off + CW == W:
            for i, (colour, row0, rows_of) in enumerate(PLANS[c]):
                s = 2 * (3 * c + i)
                links = Links(place, sems[s], sems[s + 1])
                count = 3 if colour == "z" else 5
                mine, bufs = bufs[:count], bufs[count:]
                col0 = (c * W) % FF
                where = (term.at[c], out, c * W // FF, col0, row0, rows_of, mine)
                if colour == "z":
                    stream = stream_z(links, *where)
                else:
                    stream = stream_xy(links, colour, "y" if colour == "x" else "x", *where)
                next(stream)
                active.append(stream)
    while active:
        tick()


def call(a, g, compute=True, comm=True):
    buffers, sems = [], []
    for plan in PLANS:
        for colour, _, rows in plan:
            buffers += scratch_of(colour, rows)
            sems += [pltpu.SemaphoreType.DMA((SEMS_Z if colour == "z" else SEMS_XY,))] * 2
    steps = TOKENS // KB
    return pl.pallas_call(
        functools.partial(kernel, compute, comm),
        out_shape=jax.ShapeDtypeStruct((2, D, FF), BF),
        in_specs=[pl.BlockSpec(memory_space=pl.ANY)] * 2,
        out_specs=pl.BlockSpec(memory_space=pltpu.VMEM),
        scratch_shapes=[
            pltpu.VMEM((2, TOKENS, D), BF),
            pltpu.VMEM((SLOTS, TOKENS, CW), BF),
            pltpu.VMEM((D, TOKENS), BF),
            pltpu.VMEM((D, CW), F32),
            pltpu.VMEM((CHUNKS, D, W), BF),
            pltpu.SemaphoreType.DMA((2, steps)),
            pltpu.SemaphoreType.DMA((SLOTS, steps)),
            *buffers,
            *sems,
        ],
        compiler_params=pltpu.CompilerParams(
            collective_id=0 if comm else None, has_side_effects=True, vmem_limit_bytes=60 * 1024 * 1024
        ),
        name="grad_sums",
    )(a, g)


def solution(mesh):
    def step(a, g):
        spec = P(("rep", "dp"))
        return jax.shard_map(call, mesh=mesh, in_specs=(spec, spec), out_specs=P("rep"), check_vma=False)(a, g)

    return step
```

time: 828 us -> 110 us (0.13)
  the two profiles are of different devices: /device:TPU:0 before, /device:TPU:6 now
where the time goes in v1:
time: 110 us
  Pallas kernels  104 us (95%)
  local copies, waits for them, and re-layouts  5.7 us (5%)
    pallas_call x1, Pallas kernels, call(): pl.pallas_call(functools.partial(kernel, compute, comm), out_shape=jax.Sh...  104 us
    unnamed x1, local copies, waits for them, and re-layouts  5.7 us

profile of v1, /device:TPU:6, one launch (start us, length us, event | category | flops | bytes accessed | tf_op | source)
XLA Modules:
  0.0 109.7 jit_solution(9081287037078905532)
XLA Ops:
  0.0 103.9 %grad_sums.1 = bf16[2,640,2048]{2,1,0:T(8,128)(2,1)} custom-call(bf16[1,2,4096,640]{3,2,1,0:T(8,128)(2,1)} %a_hbm.1, bf16[1,2,4096,2048]{3,2,1,0:T(8,128)(2,1)} %g_hbm.1), custom_call_target="tpu_custom_call" | custom-call | tf_op jit(solution)/shard_map/grad_sums/pallas_call | solution.py:342
  104.0 5.7 %copy.4 = bf16[2,640,2048]{2,1,0:T(8,128)(2,1)} copy(bf16[2,640,2048]{2,1,0:T(8,128)(2,1)} %grad_sums.1) | data formatting | bytes 10485760
